TPU v7x, 256 devices: a whole 4x4x8 slice. The times are simulated.
256 devices in a mesh: grp: 8 (over z_lo, core), tab: 32 (over x, z_hi, y).
Axes of the slice: x: 4, y: 4, z: 8 (z_hi: 2, z_lo: 4; z = z_hi * 4 + z_lo), core: 2. Of those that a mesh axis runs over, the one named last changes fastest.
Arguments:
- sample_ids: int32 [4, 8192, 2048], P(None, ('grp', 'tab')), may hold values from 0 to 1535
- id_weights: bfloat16 [4, 8192, 2048], P(None, ('grp', 'tab')), may hold values from 0.25 to 2
- dense_features: bfloat16 [4, 8192, 128], P(None, ('grp', 'tab')), may hold values from -6 to 6
- click_labels: int32 [4, 8192], P(None, ('grp', 'tab')), may hold values 0 or 1
- table_shards: bfloat16 [256, 1536, 128], P('tab'), may hold values from -1.1953125 to 1.1953125
- slot_table: int32 [256], replicated, may hold values from 0 to 255, each once
- top_weight: bfloat16 [256, 1024], replicated, may hold values from -0.375 to 0.375
- top_bias: float32 [1024], replicated, may hold values from -3 to 3
- out_weight: bfloat16 [1024], replicated, may hold values from -0.1875 to 0.1875
Outputs:
- logits: float32 [4, 8192], P(None, ('grp', 'tab'))
- grad_top: float32 [256, 1024], replicated
- grad_bias: float32 [1024], replicated
Inputs may be any that keep to these rules, and one draw needn't show every extreme that they name: `slot_table`: a permutation: each table stands in exactly one slot.
All inputs are finite; a program needn't handle non-finite values. No bound on the sum of `click_labels` on one device may be relied on, other than what follows from the above.
Results may differ from a plain program's by a relative error of at most 0.0056.
Values may be sent and summed in bfloat16 or wider, within the bound.
A program may use at most 128 MiB of HBM per device.

v0:
```python
import functools
import math

import jax
import jax.numpy as jnp
from jax import lax
from jax.experimental import pallas as pl
from jax.experimental.pallas import tpu as pltpu
from jax.sharding import PartitionSpec as P

HOTS = 8
LANES = 128
MESH = pl.DeviceIdType.MESH
loss_scale = 32768.0

Z_BIT = 4
PLANE = 16
ROWS = 128


def place():
    grp, tab = lax.axis_index("grp"), lax.axis_index("tab")
    return grp, tab


def mirrored(grp):
    return (3 - grp // 2) * 2 + grp % 2


def order(step):
    return (step // 8) * 8 + (step % 2) * Z_BIT + (step // 2) % 4


def flip(value, offset, bits):
    total = 0
    for bit in range(bits):
        unit = 1 << bit
        one, two = (value // unit) % 2, (offset // unit) % 2
        total = total + (one + two - 2 * one * two) * unit
    return total


def peer_of(grp, tab, offset):
    cross = (offset // Z_BIT) % 2
    there = cross * mirrored(grp) + (1 - cross) * grp
    return {"grp": there, "tab": flip(tab, offset, 5)}


def gather_rows(source, index):
    dims = lax.GatherDimensionNumbers(
        offset_dims=(),
        collapsed_slice_dims=(0,),
        start_index_map=(0,),
        operand_batching_dims=(1,),
        start_indices_batching_dims=(1,),
    )
    return lax.gather(
        source, index[..., None], dims, slice_sizes=(1, 1),
        mode=lax.GatherScatterMode.PROMISE_IN_BOUNDS,
    )


def exchange_kernel(
    slots_ref, ids_hbm, weights_hbm, features_hbm, tables_hbm, scores_ref,
    ids_ref, weights_ref, features_ref, tables_ref, ids_t, weights_t, send, recv, feats, back, summed,
    load_sem, send_sem, recv_sem, fsend_sem, frecv_sem, bsend_sem, brecv_sem,
):
    grp, tab = place()
    peers = send.shape[0]
    own_slots, vocab, width = tables_ref.shape
    lines = own_slots * HOTS
    loads = [
        pltpu.make_async_copy(source, target, load_sem.at[at])
        for at, (source, target) in enumerate(
            [(features_hbm, features_ref), (ids_hbm, ids_ref), (weights_hbm, weights_ref), (tables_hbm, tables_ref)]
        )
    ]
    for load in loads:
        load.start()
    barrier = pltpu.get_barrier_semaphore()

    def greet(offset, _):
        pl.semaphore_signal(barrier, inc=1, device_id=peer_of(grp, tab, offset), device_id_type=MESH)
        return 0

    lax.fori_loop(1, peers, greet, 0)
    loads[0].wait()
    feats[0] = features_ref[...]
    loads[1].wait()
    loads[2].wait()
    per_block = LANES // HOTS
    for at in range(ids_ref.shape[1] // LANES):
        columns = slice(at * LANES, (at + 1) * LANES)
        held = slice(at * per_block, (at + 1) * per_block)
        ids = ids_ref[:, columns]
        code = jnp.left_shift((ids & 127) + 128, jnp.right_shift(ids, 7))
        ids_t[held] = code.astype(jnp.float32).T.reshape(per_block, HOTS, LANES)
        weights_t[held] = weights_ref[:, columns].astype(jnp.float32).T.reshape(per_block, HOTS, LANES)

    def packed(offset, target):
        first = flip(tab, offset, 5) * own_slots
        for pair in range(own_slots // 2):
            one, two = slots_ref[first + 2 * pair], slots_ref[first + 2 * pair + 1]
            rows = slice(pair * 2 * HOTS, (pair + 1) * 2 * HOTS)
            target[offset, rows, :] = jnp.concatenate([ids_t[one], ids_t[two]], axis=0).astype(jnp.bfloat16)
            rows = slice(lines + pair * 2 * HOTS, lines + (pair + 1) * 2 * HOTS)
            target[offset, rows, :] = jnp.concatenate([weights_t[one], weights_t[two]], axis=0).astype(jnp.bfloat16)

    packed(0, recv)
    pl.semaphore_wait(barrier, peers - 1)

    def feature_copy(source, offset):
        return pltpu.make_async_remote_copy(
            src_ref=source, dst_ref=feats.at[offset],
            send_sem=fsend_sem.at[offset], recv_sem=frecv_sem.at[offset],
            device_id=peer_of(grp, tab, offset), device_id_type=MESH,
        )

    def passed_on(offset):
        return pltpu.make_async_remote_copy(
            src_ref=feats.at[Z_BIT], dst_ref=feats.at[offset + Z_BIT],
            send_sem=fsend_sem.at[offset + Z_BIT], recv_sem=frecv_sem.at[offset + Z_BIT],
            device_id=peer_of(grp, tab, offset), device_id_type=MESH,
        )

    def payload_copy(offset):
        return pltpu.make_async_remote_copy(
            src_ref=send.at[offset], dst_ref=recv.at[offset],
            send_sem=send_sem.at[offset], recv_sem=recv_sem.at[offset],
            device_id=peer_of(grp, tab, offset), device_id_type=MESH,
        )

    def score_copy(offset):
        return pltpu.make_async_remote_copy(
            src_ref=back.at[offset], dst_ref=scores_ref.at[tab],
            send_sem=bsend_sem.at[offset], recv_sem=brecv_sem.at[offset],
            device_id=peer_of(grp, tab, offset), device_id_type=MESH,
        )

    feature_copy(features_ref, Z_BIT).start()

    def send_features(m, _):
        feature_copy(features_ref, order(2 * m)).start()
        return 0

    lax.fori_loop(1, PLANE, send_features, 0)


    def send_payload(step, _):
        offset = order(step)
        packed(offset, send)
        payload_copy(offset).start()
        return 0

    lax.fori_loop(1, peers, send_payload, 0)
    feature_copy(features_ref, Z_BIT).wait_recv()

    def pass_features(m, _):
        passed_on(order(2 * m)).start()
        return 0

    lax.fori_loop(1, PLANE, pass_features, 0)

    scale = 1.0 / math.sqrt(width)
    tile = 128

    loads[3].wait()

    def pair_step(m, _):
        near = order(2 * m)
        far = near + Z_BIT

        @pl.when(m > 0)
        def _():
            payload_copy(near).wait_recv()
            feature_copy(features_ref, near).wait_recv()
            passed_on(near).wait_recv()

        payload_copy(far).wait_recv()
        vectors = jnp.concatenate([feats[near], feats[far]], axis=0)
        both = (near, far)

        for slot in range(own_slots):
            rows = slice(slot * HOTS, (slot + 1) * HOTS)
            low, chunk, total = [], [], []
            for source in both:
                code = recv[source, rows, :].astype(jnp.int32)
                high = jnp.zeros_like(code)
                for level in range(8, 8 + (vocab - 1) // 128):
                    high = high + (code >= (1 << level)).astype(jnp.int32)
                rest = jnp.right_shift(code, high) - 128
                low.append(rest & 7)
                chunk.append(high * 16 + jnp.right_shift(rest, 3))
                total.append(jnp.zeros((HOTS, LANES), jnp.float32))
            for part in range(vocab // tile):
                dots = lax.dot_general(
                    tables_ref[slot, part * tile : (part + 1) * tile, :], vectors,
                    (((1,), (1,)), ((), ())), preferred_element_type=jnp.float32,
                )
                for row in range(tile // HOTS):
                    at = part * (tile // HOTS) + row
                    for side in range(2):
                        found = gather_rows(
                            dots[row * HOTS : (row + 1) * HOTS, side * LANES : (side + 1) * LANES],
                            low[side],
                        )
                        total[side] = jnp.where(chunk[side] == at, found, total[side])
            weight_rows = slice(lines + slot * HOTS, lines + (slot + 1) * HOTS)
            for side, source in enumerate(both):
                weighed = total[side] * recv[source, weight_rows, :].astype(jnp.float32)
                summed[side, slot : slot + 1, :] = jnp.sum(weighed, axis=0, keepdims=True) * scale

        back[near] = summed[0].astype(jnp.bfloat16)
        back[far] = summed[1].astype(jnp.bfloat16)

        @pl.when(m > 0)
        def _():
            score_copy(near).start()

        score_copy(far).start()
        return 0

    lax.fori_loop(0, PLANE, pair_step, 0)
    scores_ref[tab] = back[0]

    def finish(offset, _):
        payload_copy(offset).wait_send()
        score_copy(offset).wait_send()
        score_copy(offset).wait_recv()
        return 0

    lax.fori_loop(1, peers, finish, 0)
    feature_copy(features_ref, Z_BIT).wait_send()

    def finish_features(m, _):
        feature_copy(features_ref, order(2 * m)).wait_send()
        passed_on(order(2 * m)).wait_send()
        return 0

    lax.fori_loop(1, PLANE, finish_features, 0)


def plane_peer(grp, tab, k):
    return {"grp": grp, "tab": flip(tab, (k // 4) * 8 + k % 4, 5)}


def column_peer(grp, tab, k):
    return {"grp": flip(grp, (k % 4) * 2, 3), "tab": flip(tab, (k // 4) * Z_BIT, 5)}


def top_kernel(
    samples_all,
    slots_ref, scores_ref, labels_ref, top_ref, bias_ref, out_ref,
    logits_ref, grad_ref, grad_bias_ref,
    grad, half_send, half_recv, plane_send, plane_recv, piece, line_send, line_recv, line_all, block, plane_all, half_all,
    bias_part, bias_half, bias_sum, bias_plane, bias_sum_two, bias_line,
    half_sem, plane_ssem, plane_rsem, line_ssem, line_rsem, lall_ssem, lall_rsem, pall_ssem, pall_rsem, hall_ssem, hall_rsem,
    bhalf_sem, bplane_ssem, bplane_rsem, bline_ssem, bline_rsem,
):
    grp, tab = place()
    core = grp % 2
    xy = (tab // 8) * 4 + tab % 4
    z = ((tab // Z_BIT) % 2) * 4 + grp // 2
    partner = {"grp": flip(grp, 1, 3), "tab": tab}
    barrier = pltpu.get_barrier_semaphore()
    pl.semaphore_signal(barrier, inc=1, device_id=partner, device_id_type=MESH)

    def greet_plane(k, _):
        pl.semaphore_signal(barrier, inc=1, device_id=plane_peer(grp, tab, k), device_id_type=MESH)
        return 0

    def greet_column(k, _):
        pl.semaphore_signal(barrier, inc=1, device_id=column_peer(grp, tab, k), device_id_type=MESH)
        return 0

    lax.fori_loop(1, 16, greet_plane, 0)
    lax.fori_loop(1, 8, greet_column, 0)

    tables, hidden_size = top_ref.shape
    at_table = (lax.broadcasted_iota(jnp.int32, (tables, tables), 0) == slots_ref[...]).astype(jnp.bfloat16)
    scores_wide = jnp.dot(at_table, scores_ref[...], preferred_element_type=jnp.float32)
    scores_t = scores_wide.astype(jnp.bfloat16)
    scores = scores_wide.T.astype(jnp.bfloat16)
    pre = jnp.dot(scores, top_ref[...], preferred_element_type=jnp.float32) + bias_ref[...]
    gate = jax.nn.sigmoid(pre)
    hidden = (pre * gate).astype(jnp.bfloat16)
    out_row = out_ref[...]
    out_wide = out_row.astype(jnp.float32)
    logit_column = jnp.sum(hidden.astype(jnp.float32) * out_wide, axis=1, keepdims=True)
    logits_ref[...] = logit_column
    delta = (jax.nn.sigmoid(logit_column) - labels_ref[...].astype(jnp.float32)) * (loss_scale / samples_all)
    slope = gate * (1.0 + pre * (1.0 - gate))
    hidden_grad_wide = delta * out_wide * slope
    hidden_grad = hidden_grad_wide.astype(jnp.bfloat16)
    grad[...] = jnp.dot(scores_t, hidden_grad, preferred_element_type=jnp.float32)
    bias_part[...] = jnp.sum(hidden_grad.astype(jnp.float32), axis=0, keepdims=True)

    other = pl.multiple_of((1 - core) * ROWS, ROWS)
    mine = pl.multiple_of(core * ROWS, ROWS)
    half_send[...] = grad[pl.ds(other, ROWS), :].reshape(16, 8, hidden_size).astype(jnp.bfloat16)

    pl.semaphore_wait(barrier, 1 + 15 + 7)

    def to_partner(source, target, sems):
        return pltpu.make_async_remote_copy(
            src_ref=source, dst_ref=target, send_sem=sems.at[0], recv_sem=sems.at[1],
            device_id=partner, device_id_type=MESH,
        )

    bias_swap = to_partner(bias_part, bias_half, bhalf_sem)
    half_swap = to_partner(half_send, half_recv, half_sem)
    bias_swap.start()
    half_swap.start()
    bias_swap.wait()
    bias_sum[...] = bias_part[...] + bias_half[...]
    bias_plane[pl.ds(xy, 1)] = bias_sum[...][None]

    def bias_to_plane(k):
        return pltpu.make_async_remote_copy(
            src_ref=bias_sum, dst_ref=bias_plane.at[xy],
            send_sem=bplane_ssem.at[k], recv_sem=bplane_rsem.at[k],
            device_id=plane_peer(grp, tab, k), device_id_type=MESH,
        )

    def grad_to_plane(k):
        return pltpu.make_async_remote_copy(
            src_ref=plane_send.at[k], dst_ref=plane_recv.at[k],
            send_sem=plane_ssem.at[k], recv_sem=plane_rsem.at[k],
            device_id=plane_peer(grp, tab, k), device_id_type=MESH,
        )

    half_swap.wait()

    def fold(k):
        row = pl.multiple_of(flip(xy, k, 4) * 8, 8)
        wide = half_recv[pl.ds(flip(xy, k, 4), 1)][0].astype(jnp.float32)
        return grad[pl.ds(pl.multiple_of(mine + row, 8), 8), :] + wide

    def send_plane(k, _):
        plane_send[k] = fold(k).astype(jnp.bfloat16)
        grad_to_plane(k).start()
        bias_to_plane(k).start()
        return 0

    lax.fori_loop(1, 16, send_plane, 0)
    piece[...] = fold(0)

    def add_plane(k, _):
        grad_to_plane(k).wait_recv()
        bias_to_plane(k).wait_recv()
        piece[...] += plane_recv[k].astype(jnp.float32)
        return 0

    lax.fori_loop(1, 16, add_plane, 0)

    total = bias_plane[0]
    for k in range(1, 16):
        total = total + bias_plane[k]
    bias_sum_two[...] = total
    bias_line[pl.ds(z, 1)] = total[None]

    def bias_to_line(k):
        return pltpu.make_async_remote_copy(
            src_ref=bias_sum_two, dst_ref=bias_line.at[z],
            send_sem=bline_ssem.at[k], recv_sem=bline_rsem.at[k],
            device_id=column_peer(grp, tab, k), device_id_type=MESH,
        )

    def grad_to_line(k):
        return pltpu.make_async_remote_copy(
            src_ref=line_send.at[k], dst_ref=line_recv.at[k],
            send_sem=line_ssem.at[k], recv_sem=line_rsem.at[k],
            device_id=column_peer(grp, tab, k), device_id_type=MESH,
        )

    def columns(k):
        return pl.ds(pl.multiple_of(flip(z, k, 3) * LANES, LANES), LANES)

    for k in range(1, 8):
        line_send[k] = piece[:, columns(k)]
        grad_to_line(k).start()
        bias_to_line(k).start()
    final = piece[:, columns(0)]
    for k in range(1, 8):
        grad_to_line(k).wait_recv()
        final = final + line_recv[k]
    line_all[0] = final

    def final_to_line(k):
        return pltpu.make_async_remote_copy(
            src_ref=line_all.at[0], dst_ref=line_all.at[k],
            send_sem=lall_ssem.at[k], recv_sem=lall_rsem.at[k],
            device_id=column_peer(grp, tab, k), device_id_type=MESH,
        )

    for k in range(1, 8):
        final_to_line(k).start()
    for k in range(1, 8):
        bias_to_line(k).wait_recv()
    total = bias_line[0]
    for k in range(1, 8):
        total = total + bias_line[k]
    grad_bias_ref[...] = total
    block[:, columns(0)] = final
    for k in range(1, 8):
        final_to_line(k).wait_recv()
        block[:, columns(k)] = line_all[k]
    plane_all[0] = block[...].astype(jnp.bfloat16)

    def block_to_plane(k):
        return pltpu.make_async_remote_copy(
            src_ref=plane_all.at[0], dst_ref=plane_all.at[k],
            send_sem=pall_ssem.at[k], recv_sem=pall_rsem.at[k],
            device_id=plane_peer(grp, tab, k), device_id_type=MESH,
        )

    def block_to_partner(k):
        return pltpu.make_async_remote_copy(
            src_ref=plane_all.at[k], dst_ref=half_all.at[k],
            send_sem=hall_ssem.at[k], recv_sem=hall_rsem.at[k],
            device_id=partner, device_id_type=MESH,
        )

    def start_blocks(k, _):
        block_to_plane(k).start()
        return 0

    lax.fori_loop(1, 16, start_blocks, 0)
    block_to_partner(0).start()

    def put(k, start, source):
        row = pl.multiple_of(start + flip(xy, k, 4) * 8, 8)
        grad_ref[pl.ds(row, 8), :] = source[k].astype(jnp.float32)

    put(0, mine, plane_all)

    def take_blocks(k, _):
        block_to_plane(k).wait_recv()
        block_to_partner(k).start()
        put(k, mine, plane_all)
        return 0

    lax.fori_loop(1, 16, take_blocks, 0)

    def take_halves(k, _):
        block_to_partner(k).wait_recv()
        put(k, other, half_all)
        block_to_partner(k).wait_send()
        return 0

    lax.fori_loop(0, 16, take_halves, 0)

    def finish_plane(k, _):
        grad_to_plane(k).wait_send()
        bias_to_plane(k).wait_send()
        block_to_plane(k).wait_send()
        return 0

    lax.fori_loop(1, 16, finish_plane, 0)
    for k in range(1, 8):
        grad_to_line(k).wait_send()
        bias_to_line(k).wait_send()
        final_to_line(k).wait_send()


def per_device(
    sample_ids, id_weights, dense_features, click_labels, table_shards, slot_table, top_weight, top_bias, out_weight,
):
    micro, local, columns = sample_ids.shape
    count = micro * local
    width = dense_features.shape[2]
    own_slots, vocab, _ = table_shards.shape
    tables, hidden_size = top_weight.shape
    peers = tables // own_slots
    samples_all = count * lax.axis_size("grp") * peers
    vmem, smem = pl.BlockSpec(memory_space=pltpu.VMEM), pl.BlockSpec(memory_space=pltpu.SMEM)
    anywhere = pl.BlockSpec(memory_space=pl.ANY)
    dma = pltpu.SemaphoreType.DMA
    bf16, f32 = jnp.bfloat16, jnp.float32

    scores = pl.pallas_call(
        exchange_kernel,
        out_shape=jax.ShapeDtypeStruct((peers, own_slots, count), bf16),
        in_specs=[smem, anywhere, anywhere, anywhere, anywhere],
        out_specs=vmem,
        scratch_shapes=[
            pltpu.VMEM((count, columns), jnp.int32),
            pltpu.VMEM((count, columns), bf16),
            pltpu.VMEM((count, width), bf16),
            pltpu.VMEM((own_slots, vocab, width), bf16),
            pltpu.VMEM((tables, HOTS, count), f32),
            pltpu.VMEM((tables, HOTS, count), f32),
            pltpu.VMEM((peers, 2 * own_slots * HOTS, count), bf16),
            pltpu.VMEM((peers, 2 * own_slots * HOTS, count), bf16),
            pltpu.VMEM((peers, count, width), bf16),
            pltpu.VMEM((peers, own_slots, count), bf16),
            pltpu.VMEM((2, own_slots, count), f32),
            dma((4,)),
        ] + [dma((peers,)) for _ in range(6)],
        compiler_params=pltpu.CompilerParams(collective_id=0, has_side_effects=True, vmem_limit_bytes=60 << 20),
        name="exchange",
    )(
        slot_table,
        sample_ids.reshape(count, columns),
        id_weights.reshape(count, columns),
        dense_features.reshape(count, width),
        table_shards,
    )

    logits, grad_top, grad_bias = pl.pallas_call(
        functools.partial(top_kernel, samples_all),
        out_shape=(
            jax.ShapeDtypeStruct((count, 1), f32),
            jax.ShapeDtypeStruct((tables, hidden_size), f32),
            jax.ShapeDtypeStruct((1, hidden_size), f32),
        ),
        in_specs=[vmem] * 6,
        out_specs=(vmem, vmem, vmem),
        scratch_shapes=[
            pltpu.VMEM((tables, hidden_size), f32),
            pltpu.VMEM((16, 8, hidden_size), bf16),
            pltpu.VMEM((16, 8, hidden_size), bf16),
            pltpu.VMEM((16, 8, hidden_size), bf16),
            pltpu.VMEM((16, 8, hidden_size), bf16),
            pltpu.VMEM((8, hidden_size), f32),
            pltpu.VMEM((8, 8, LANES), f32),
            pltpu.VMEM((8, 8, LANES), f32),
            pltpu.VMEM((8, 8, LANES), f32),
            pltpu.VMEM((8, hidden_size), f32),
            pltpu.VMEM((16, 8, hidden_size), bf16),
            pltpu.VMEM((16, 8, hidden_size), bf16),
            pltpu.VMEM((1, hidden_size), f32),
            pltpu.VMEM((1, hidden_size), f32),
            pltpu.VMEM((1, hidden_size), f32),
            pltpu.VMEM((16, 1, hidden_size), f32),
            pltpu.VMEM((1, hidden_size), f32),
            pltpu.VMEM((8, 1, hidden_size), f32),
            dma((2,)), dma((16,)), dma((16,)), dma((8,)), dma((8,)), dma((8,)), dma((8,)),
            dma((16,)), dma((16,)), dma((16,)), dma((16,)),
            dma((2,)), dma((16,)), dma((16,)), dma((8,)), dma((8,)),
        ],
        compiler_params=pltpu.CompilerParams(collective_id=1, has_side_effects=True, vmem_limit_bytes=48 << 20),
        name="top",
    )(
        slot_table.reshape(1, tables),
        scores.reshape(tables, count),
        click_labels.reshape(count, 1),
        top_weight,
        top_bias.reshape(1, hidden_size),
        out_weight.reshape(1, hidden_size),
    )
    return logits.reshape(micro, local), grad_top, grad_bias.reshape(hidden_size)


def solution(mesh):
    return jax.shard_map(
        per_device,
        mesh=mesh,
        in_specs=(
            P(None, ("grp", "tab"), None),
            P(None, ("grp", "tab"), None),
            P(None, ("grp", "tab"), None),
            P(None, ("grp", "tab")),
            P("tab", None, None),
            P(),
            P(),
            P(),
            P(),
        ),
        out_specs=(P(None, ("grp", "tab")), P(), P()),
        check_vma=False,
    )
```

profile of v0, /device:TPU:1, one launch (start us, length us, event | category | flops | bytes accessed | tf_op | source)
XLA Modules:
  0.0 110.6 jit_solution(7635990238173335789)
XLA Ops:
  0.6 0.0 copy-start.3
  0.6 0.0 copy-start.2
  0.7 0.0 copy-start
  0.7 0.0 copy-start.4
  0.7 0.8 reshape.43.out_ref
  1.4 65.1 %exchange.1 = bf16[32,8,128]{2,1,0:T(8,128)(2,1)} custom-call(s32[256]{0:T(256)} %slots_ref.1, s32[128,2048]{1,0:T(8,128)} %bitcast.11, bf16[128,2048]{1,0:T(8,128)(2,1)} %bitcast.12, bf16[128,128]{1,0:T(8,128)(2,1)} %bitcast.13, bf16[8,1536,128]{2,1,0:T(8,128)(2,1)} %tables_hbm.1), custom_call_target="tpu_custom_call" | custom-call | tf_op jit(solution)/shard_map/exchange/pallas_call | solution.py:481
  66.6 0.0 copy-done.4
  66.6 0.1 reshape.46.labels_ref
  66.7 0.0 copy-done.3
  66.7 0.0 copy-done.2
  66.7 0.0 copy-done
  66.7 0.0 copy-start.1
  66.7 0.8 copy-done.1
  67.5 40.7 %top.1 = (f32[128,1]{1,0:T(8,128)S(1)}, f32[256,1024]{1,0:T(8,128)S(1)}, f32[1,1024]{1,0:T(1,128)S(1)}) custom-call(s32[1,256]{1,0:T(1,128)S(1)} %bitcast.10, bf16[256,128]{1,0:T(8,128)(2,1)S(1)} %bitcast.7, s32[128,1]{1,0:T(8,128)S(1)} %reshape.46.labels_ref, bf16[256,1024]{1,0:T(8,128)(2,1)S(1)} %copy-done, f32[1,1024]{1,0:T(1,128)S(1)} %bitcast.9, ...), custom_call_target="tpu_custom_call" | custom-call | tf_op jit(solution)/shard_map/top/pallas_call | solution.py:510
  108.2 0.1 reduce
  108.3 0.7 reshape.44
  109.0 1.0 copy.16
  110.0 0.6 copy.17
Async XLA Ops:
  0.6 66.0 %copy-start.3 = (s32[256]{0:T(256)S(1)}, s32[256]{0:T(256)}, u32[]{:S(2)}) copy-start(s32[256]{0:T(256)} %slots_ref.1) | copy-start | bytes 3076
  0.6 66.0 %copy-start.2 = (f32[1024]{0:T(1024)S(1)}, f32[1024]{0:T(1024)}, u32[]{:S(2)}) copy-start(f32[1024]{0:T(1024)} %param.16) | copy-start | bytes 12292
  0.7 66.0 %copy-start = (bf16[256,1024]{1,0:T(8,128)(2,1)S(1)}, bf16[256,1024]{1,0:T(8,128)(2,1)}, u32[]{:S(2)}) copy-start(bf16[256,1024]{1,0:T(8,128)(2,1)} %top_ref.1) | copy-start | bytes 1572868
  0.7 65.9 %copy-start.4 = (s32[4,32]{1,0:T(4,128)S(1)}, s32[4,32]{1,0:T(4,128)}, u32[]{:S(2)}) copy-start(s32[4,32]{1,0:T(4,128)} %param.12) | copy-start | bytes 1540
  66.7 0.8 copy-start.1
where the time goes:
time: 111 us
  Pallas kernels  106 us (95%)
  local copies, waits for them, and re-layouts  3.94 us (4%)
    pallas_call x1, Pallas kernels, per_device(): pl.pallas_call(exchange_kernel, out_shape=jax.ShapeDtypeStruct((peers, ow...  65.1 us
    pallas_call x1, Pallas kernels, per_device(): pl.pallas_call(functools.partial(top_kernel, samples_all), out_shape=(jax...  40.7 us
    unnamed x12, local copies, waits for them, and re-layouts  2.41 us

commit v1 on v0

--- a/solution.py
+++ b/solution.py
@@ -29,6 +29,10 @@
 
 def order(step):
     return (step // 8) * 8 + (step % 2) * Z_BIT + (step // 2) % 4
+
+
+def plane(at):
+    return (at // 4) * 8 + at % 4
 
 
 def flip(value, offset, bits):
@@ -60,10 +64,25 @@
     )
 
 
-def exchange_kernel(
-    slots_ref, ids_hbm, weights_hbm, features_hbm, tables_hbm, scores_ref,
-    ids_ref, weights_ref, features_ref, tables_ref, ids_t, weights_t, send, recv, feats, back, summed,
+def plane_peer(grp, tab, k):
+    return {"grp": grp, "tab": flip(tab, (k // 4) * 8 + k % 4, 5)}
+
+
+def column_peer(grp, tab, k):
+    return {"grp": flip(grp, (k % 4) * 2, 3), "tab": flip(tab, (k // 4) * Z_BIT, 5)}
+
+
+def step_kernel(
+    samples_all,
+    slots_ref, slots_hbm, ids_hbm, weights_hbm, features_hbm, tables_hbm, labels_hbm, top_hbm, bias_hbm, out_hbm,
+    logits_ref, grad_ref, grad_bias_ref,
+    ids_ref, weights_ref, features_ref, tables_ref, slot_row, labels_ref, top_ref, bias_ref, out_ref,
+    ids_t, weights_t, send, recv, feats, back, summed, scores_ref,
+    grad, half_send, half_recv, plane_send, plane_recv, piece, line_send, line_recv, plane_all, half_all,
+    bias_part, bias_half, bias_sum, bias_plane, bias_sum_two, bias_line,
     load_sem, send_sem, recv_sem, fsend_sem, frecv_sem, bsend_sem, brecv_sem,
+    half_sem, plane_ssem, plane_rsem, line_ssem, line_rsem, pall_ssem, pall_rsem, hall_ssem, hall_rsem,
+    bhalf_sem, bplane_ssem, bplane_rsem, bline_ssem, bline_rsem,
 ):
     grp, tab = place()
     peers = send.shape[0]
@@ -72,7 +91,10 @@
     loads = [
         pltpu.make_async_copy(source, target, load_sem.at[at])
         for at, (source, target) in enumerate(
-            [(features_hbm, features_ref), (ids_hbm, ids_ref), (weights_hbm, weights_ref), (tables_hbm, tables_ref)]
+            [
+                (features_hbm, features_ref), (ids_hbm, ids_ref), (weights_hbm, weights_ref), (tables_hbm, tables_ref),
+                (slots_hbm, slot_row), (labels_hbm, labels_ref), (top_hbm, top_ref), (bias_hbm, bias_ref), (out_hbm, out_ref),
+            ]
         )
     ]
     for load in loads:
@@ -83,7 +105,14 @@
         pl.semaphore_signal(barrier, inc=1, device_id=peer_of(grp, tab, offset), device_id_type=MESH)
         return 0
 
+    def greet_column(k, _):
+        pl.semaphore_signal(barrier, inc=1, device_id=column_peer(grp, tab, k), device_id_type=MESH)
+        return 0
+
+    partner = {"grp": flip(grp, 1, 3), "tab": tab}
     lax.fori_loop(1, peers, greet, 0)
+    lax.fori_loop(1, 8, greet_column, 0)
+    pl.semaphore_signal(barrier, inc=1, device_id=partner, device_id_type=MESH)
     loads[0].wait()
     feats[0] = features_ref[...]
     loads[1].wait()
@@ -107,7 +136,7 @@
             target[offset, rows, :] = jnp.concatenate([weights_t[one], weights_t[two]], axis=0).astype(jnp.bfloat16)
 
     packed(0, recv)
-    pl.semaphore_wait(barrier, peers - 1)
+    pl.semaphore_wait(barrier, peers - 1 + 7 + 1)
 
     def feature_copy(source, offset):
         return pltpu.make_async_remote_copy(
@@ -153,32 +182,29 @@
         return 0
 
     lax.fori_loop(1, peers, send_payload, 0)
-    feature_copy(features_ref, Z_BIT).wait_recv()
-
     def pass_features(m, _):
         passed_on(order(2 * m)).start()
         return 0
 
-    lax.fori_loop(1, PLANE, pass_features, 0)
-
     scale = 1.0 / math.sqrt(width)
     tile = 128
 
     loads[3].wait()
 
     def pair_step(m, _):
-        near = order(2 * m)
-        far = near + Z_BIT
+        both = [plane(2 * (m % 8) + side) + (m // 8) * Z_BIT for side in range(2)]
 
         @pl.when(m > 0)
         def _():
-            payload_copy(near).wait_recv()
-            feature_copy(features_ref, near).wait_recv()
-            passed_on(near).wait_recv()
-
-        payload_copy(far).wait_recv()
-        vectors = jnp.concatenate([feats[near], feats[far]], axis=0)
-        both = (near, far)
+            payload_copy(both[0]).wait_recv()
+
+        @pl.when(m % 8 > 0)
+        def _():
+            feature_copy(features_ref, both[0]).wait_recv()
+
+        payload_copy(both[1]).wait_recv()
+        feature_copy(features_ref, both[1]).wait_recv()
+        vectors = jnp.concatenate([feats[both[0]], feats[both[1]]], axis=0)
 
         for slot in range(own_slots):
             rows = slice(slot * HOTS, (slot + 1) * HOTS)
@@ -210,85 +236,64 @@
                 weighed = total[side] * recv[source, weight_rows, :].astype(jnp.float32)
                 summed[side, slot : slot + 1, :] = jnp.sum(weighed, axis=0, keepdims=True) * scale
 
-        back[near] = summed[0].astype(jnp.bfloat16)
-        back[far] = summed[1].astype(jnp.bfloat16)
+        for side in range(2):
+            back[both[side]] = summed[side].astype(jnp.bfloat16)
 
         @pl.when(m > 0)
         def _():
-            score_copy(near).start()
-
-        score_copy(far).start()
+            score_copy(both[0]).start()
+
+        score_copy(both[1]).start()
+
+        @pl.when(m == 0)
+        def _():
+            feature_copy(features_ref, Z_BIT).wait_recv()
+            lax.fori_loop(1, PLANE, pass_features, 0)
+
         return 0
 
     lax.fori_loop(0, PLANE, pair_step, 0)
     scores_ref[tab] = back[0]
 
-    def finish(offset, _):
-        payload_copy(offset).wait_send()
-        score_copy(offset).wait_send()
+    for load in loads[4:]:
+        load.wait()
+
+    def take_scores(offset, _):
         score_copy(offset).wait_recv()
         return 0
 
-    lax.fori_loop(1, peers, finish, 0)
-    feature_copy(features_ref, Z_BIT).wait_send()
-
-    def finish_features(m, _):
-        feature_copy(features_ref, order(2 * m)).wait_send()
-        passed_on(order(2 * m)).wait_send()
-        return 0
-
-    lax.fori_loop(1, PLANE, finish_features, 0)
-
-
-def plane_peer(grp, tab, k):
-    return {"grp": grp, "tab": flip(tab, (k // 4) * 8 + k % 4, 5)}
-
-
-def column_peer(grp, tab, k):
-    return {"grp": flip(grp, (k % 4) * 2, 3), "tab": flip(tab, (k // 4) * Z_BIT, 5)}
-
-
-def top_kernel(
-    samples_all,
-    slots_ref, scores_ref, labels_ref, top_ref, bias_ref, out_ref,
-    logits_ref, grad_ref, grad_bias_ref,
-    grad, half_send, half_recv, plane_send, plane_recv, piece, line_send, line_recv, line_all, block, plane_all, half_all,
-    bias_part, bias_half, bias_sum, bias_plane, bias_sum_two, bias_line,
-    half_sem, plane_ssem, plane_rsem, line_ssem, line_rsem, lall_ssem, lall_rsem, pall_ssem, pall_rsem, hall_ssem, hall_rsem,
-    bhalf_sem, bplane_ssem, bplane_rsem, bline_ssem, bline_rsem,
-):
-    grp, tab = place()
+    lax.fori_loop(1, peers, take_scores, 0)
+
     core = grp % 2
     xy = (tab // 8) * 4 + tab % 4
     z = ((tab // Z_BIT) % 2) * 4 + grp // 2
-    partner = {"grp": flip(grp, 1, 3), "tab": tab}
-    barrier = pltpu.get_barrier_semaphore()
-    pl.semaphore_signal(barrier, inc=1, device_id=partner, device_id_type=MESH)
-
-    def greet_plane(k, _):
-        pl.semaphore_signal(barrier, inc=1, device_id=plane_peer(grp, tab, k), device_id_type=MESH)
-        return 0
-
-    def greet_column(k, _):
-        pl.semaphore_signal(barrier, inc=1, device_id=column_peer(grp, tab, k), device_id_type=MESH)
-        return 0
-
-    lax.fori_loop(1, 16, greet_plane, 0)
-    lax.fori_loop(1, 8, greet_column, 0)
-
     tables, hidden_size = top_ref.shape
-    at_table = (lax.broadcasted_iota(jnp.int32, (tables, tables), 0) == slots_ref[...]).astype(jnp.bfloat16)
-    scores_wide = jnp.dot(at_table, scores_ref[...], preferred_element_type=jnp.float32)
+    at_table = (lax.broadcasted_iota(jnp.int32, (tables, tables), 0) == slot_row[...]).astype(jnp.bfloat16)
+    scores_wide = jnp.dot(at_table, scores_ref[...].reshape(tables, LANES), preferred_element_type=jnp.float32)
     scores_t = scores_wide.astype(jnp.bfloat16)
     scores = scores_wide.T.astype(jnp.bfloat16)
     pre = jnp.dot(scores, top_ref[...], preferred_element_type=jnp.float32) + bias_ref[...]
     gate = jax.nn.sigmoid(pre)
     hidden = (pre * gate).astype(jnp.bfloat16)
-    out_row = out_ref[...]
-    out_wide = out_row.astype(jnp.float32)
+    out_wide = out_ref[...].astype(jnp.float32).reshape(1, hidden_size)
     logit_column = jnp.sum(hidden.astype(jnp.float32) * out_wide, axis=1, keepdims=True)
-    logits_ref[...] = logit_column
-    delta = (jax.nn.sigmoid(logit_column) - labels_ref[...].astype(jnp.float32)) * (loss_scale / samples_all)
+    micro, local = labels_ref.shape
+    sample = lax.broadcasted_iota(jnp.int32, (LANES, local), 0)
+    within = sample % local == lax.broadcasted_iota(jnp.int32, (LANES, local), 1)
+    batch_of = lax.broadcasted_iota(jnp.int32, (LANES, micro), 0) // local
+    spread = lax.dot_general(
+        within.astype(jnp.float32), labels_ref[...].astype(jnp.float32),
+        (((1,), (1,)), ((), ())), preferred_element_type=jnp.float32,
+    )
+    own_batch = batch_of == lax.broadcasted_iota(jnp.int32, (LANES, micro), 1)
+    labels = jnp.sum(jnp.where(own_batch, spread, 0.0), axis=1, keepdims=True)
+    rows_of = lax.broadcasted_iota(jnp.int32, (micro, LANES), 1) // local
+    picks = (rows_of == lax.broadcasted_iota(jnp.int32, (micro, LANES), 0)).astype(jnp.float32)
+    logits_ref[...] = jnp.dot(
+        picks, jnp.where(within, logit_column, 0.0),
+        precision=lax.Precision.HIGHEST, preferred_element_type=jnp.float32,
+    )
+    delta = (jax.nn.sigmoid(logit_column) - labels) * (loss_scale / samples_all)
     slope = gate * (1.0 + pre * (1.0 - gate))
     hidden_grad_wide = delta * out_wide * slope
     hidden_grad = hidden_grad_wide.astype(jnp.bfloat16)
@@ -298,8 +303,6 @@
     other = pl.multiple_of((1 - core) * ROWS, ROWS)
     mine = pl.multiple_of(core * ROWS, ROWS)
     half_send[...] = grad[pl.ds(other, ROWS), :].reshape(16, 8, hidden_size).astype(jnp.bfloat16)
-
-    pl.semaphore_wait(barrier, 1 + 15 + 7)
 
     def to_partner(source, target, sems):
         return pltpu.make_async_remote_copy(
@@ -353,6 +356,17 @@
 
     lax.fori_loop(1, 16, add_plane, 0)
 
+    def grad_to_line(k):
+        return pltpu.make_async_remote_copy(
+            src_ref=line_send, dst_ref=line_recv.at[z],
+            send_sem=line_ssem.at[k], recv_sem=line_rsem.at[k],
+            device_id=column_peer(grp, tab, k), device_id_type=MESH,
+        )
+
+    line_send[...] = piece[...].astype(jnp.bfloat16)
+    line_recv[pl.ds(z, 1)] = piece[...].astype(jnp.bfloat16)[None]
+    for k in range(1, 8):
+        grad_to_line(k).start()
     total = bias_plane[0]
     for k in range(1, 16):
         total = total + bias_plane[k]
@@ -366,46 +380,14 @@
             device_id=column_peer(grp, tab, k), device_id_type=MESH,
         )
 
-    def grad_to_line(k):
-        return pltpu.make_async_remote_copy(
-            src_ref=line_send.at[k], dst_ref=line_recv.at[k],
-            send_sem=line_ssem.at[k], recv_sem=line_rsem.at[k],
-            device_id=column_peer(grp, tab, k), device_id_type=MESH,
-        )
-
-    def columns(k):
-        return pl.ds(pl.multiple_of(flip(z, k, 3) * LANES, LANES), LANES)
-
-    for k in range(1, 8):
-        line_send[k] = piece[:, columns(k)]
-        grad_to_line(k).start()
+    for k in range(1, 8):
         bias_to_line(k).start()
-    final = piece[:, columns(0)]
     for k in range(1, 8):
         grad_to_line(k).wait_recv()
-        final = final + line_recv[k]
-    line_all[0] = final
-
-    def final_to_line(k):
-        return pltpu.make_async_remote_copy(
-            src_ref=line_all.at[0], dst_ref=line_all.at[k],
-            send_sem=lall_ssem.at[k], recv_sem=lall_rsem.at[k],
-            device_id=column_peer(grp, tab, k), device_id_type=MESH,
-        )
-
-    for k in range(1, 8):
-        final_to_line(k).start()
-    for k in range(1, 8):
-        bias_to_line(k).wait_recv()
-    total = bias_line[0]
-    for k in range(1, 8):
-        total = total + bias_line[k]
-    grad_bias_ref[...] = total
-    block[:, columns(0)] = final
-    for k in range(1, 8):
-        final_to_line(k).wait_recv()
-        block[:, columns(k)] = line_all[k]
-    plane_all[0] = block[...].astype(jnp.bfloat16)
+    block = line_recv[0].astype(jnp.float32)
+    for k in range(1, 8):
+        block = block + line_recv[k].astype(jnp.float32)
+    plane_all[0] = block.astype(jnp.bfloat16)
 
     def block_to_plane(k):
         return pltpu.make_async_remote_copy(
@@ -427,6 +409,12 @@
 
     lax.fori_loop(1, 16, start_blocks, 0)
     block_to_partner(0).start()
+    for k in range(1, 8):
+        bias_to_line(k).wait_recv()
+    total = bias_line[0]
+    for k in range(1, 8):
+        total = total + bias_line[k]
+    grad_bias_ref[...] = total
 
     def put(k, start, source):
         row = pl.multiple_of(start + flip(xy, k, 4) * 8, 8)
@@ -460,7 +448,21 @@
     for k in range(1, 8):
         grad_to_line(k).wait_send()
         bias_to_line(k).wait_send()
-        final_to_line(k).wait_send()
+
+    def finish(offset, _):
+        payload_copy(offset).wait_send()
+        score_copy(offset).wait_send()
+        return 0
+
+    lax.fori_loop(1, peers, finish, 0)
+    feature_copy(features_ref, Z_BIT).wait_send()
+
+    def finish_features(m, _):
+        feature_copy(features_ref, order(2 * m)).wait_send()
+        passed_on(order(2 * m)).wait_send()
+        return 0
+
+    lax.fori_loop(1, PLANE, finish_features, 0)
 
 
 def per_device(
@@ -478,16 +480,25 @@
     dma = pltpu.SemaphoreType.DMA
     bf16, f32 = jnp.bfloat16, jnp.float32
 
-    scores = pl.pallas_call(
-        exchange_kernel,
-        out_shape=jax.ShapeDtypeStruct((peers, own_slots, count), bf16),
-        in_specs=[smem, anywhere, anywhere, anywhere, anywhere],
-        out_specs=vmem,
+    logits, grad_top, grad_bias = pl.pallas_call(
+        functools.partial(step_kernel, samples_all),
+        out_shape=(
+            jax.ShapeDtypeStruct((micro, local), f32),
+            jax.ShapeDtypeStruct((tables, hidden_size), f32),
+            jax.ShapeDtypeStruct((1, hidden_size), f32),
+        ),
+        in_specs=[smem] + [anywhere] * 9,
+        out_specs=(vmem, vmem, vmem),
         scratch_shapes=[
             pltpu.VMEM((count, columns), jnp.int32),
             pltpu.VMEM((count, columns), bf16),
             pltpu.VMEM((count, width), bf16),
             pltpu.VMEM((own_slots, vocab, width), bf16),
+            pltpu.VMEM((1, tables), jnp.int32),
+            pltpu.VMEM((micro, local), jnp.int32),
+            pltpu.VMEM((tables, hidden_size), bf16),
+            pltpu.VMEM((1, hidden_size), f32),
+            pltpu.VMEM((hidden_size,), bf16),
             pltpu.VMEM((tables, HOTS, count), f32),
             pltpu.VMEM((tables, HOTS, count), f32),
             pltpu.VMEM((peers, 2 * own_slots * HOTS, count), bf16),
@@ -495,38 +506,15 @@
             pltpu.VMEM((peers, count, width), bf16),
             pltpu.VMEM((peers, own_slots, count), bf16),
             pltpu.VMEM((2, own_slots, count), f32),
-            dma((4,)),
-        ] + [dma((peers,)) for _ in range(6)],
-        compiler_params=pltpu.CompilerParams(collective_id=0, has_side_effects=True, vmem_limit_bytes=60 << 20),
-        name="exchange",
-    )(
-        slot_table,
-        sample_ids.reshape(count, columns),
-        id_weights.reshape(count, columns),
-        dense_features.reshape(count, width),
-        table_shards,
-    )
-
-    logits, grad_top, grad_bias = pl.pallas_call(
-        functools.partial(top_kernel, samples_all),
-        out_shape=(
-            jax.ShapeDtypeStruct((count, 1), f32),
-            jax.ShapeDtypeStruct((tables, hidden_size), f32),
-            jax.ShapeDtypeStruct((1, hidden_size), f32),
-        ),
-        in_specs=[vmem] * 6,
-        out_specs=(vmem, vmem, vmem),
-        scratch_shapes=[
+            pltpu.VMEM((peers, own_slots, count), bf16),
             pltpu.VMEM((tables, hidden_size), f32),
             pltpu.VMEM((16, 8, hidden_size), bf16),
             pltpu.VMEM((16, 8, hidden_size), bf16),
             pltpu.VMEM((16, 8, hidden_size), bf16),
             pltpu.VMEM((16, 8, hidden_size), bf16),
             pltpu.VMEM((8, hidden_size), f32),
-            pltpu.VMEM((8, 8, LANES), f32),
-            pltpu.VMEM((8, 8, LANES), f32),
-            pltpu.VMEM((8, 8, LANES), f32),
-            pltpu.VMEM((8, hidden_size), f32),
+            pltpu.VMEM((8, hidden_size), bf16),
+            pltpu.VMEM((8, 8, hidden_size), bf16),
             pltpu.VMEM((16, 8, hidden_size), bf16),
             pltpu.VMEM((16, 8, hidden_size), bf16),
             pltpu.VMEM((1, hidden_size), f32),
@@ -535,21 +523,27 @@
             pltpu.VMEM((16, 1, hidden_size), f32),
             pltpu.VMEM((1, hidden_size), f32),
             pltpu.VMEM((8, 1, hidden_size), f32),
-            dma((2,)), dma((16,)), dma((16,)), dma((8,)), dma((8,)), dma((8,)), dma((8,)),
+            dma((9,)),
+        ] + [dma((peers,)) for _ in range(6)] + [
+            dma((2,)), dma((16,)), dma((16,)), dma((8,)), dma((8,)),
             dma((16,)), dma((16,)), dma((16,)), dma((16,)),
             dma((2,)), dma((16,)), dma((16,)), dma((8,)), dma((8,)),
         ],
-        compiler_params=pltpu.CompilerParams(collective_id=1, has_side_effects=True, vmem_limit_bytes=48 << 20),
-        name="top",
+        compiler_params=pltpu.CompilerParams(collective_id=0, has_side_effects=True, vmem_limit_bytes=60 << 20),
+        name="step",
     )(
+        slot_table,
         slot_table.reshape(1, tables),
-        scores.reshape(tables, count),
-        click_labels.reshape(count, 1),
+        sample_ids.reshape(count, columns),
+        id_weights.reshape(count, columns),
+        dense_features.reshape(count, width),
+        table_shards,
+        click_labels,
         top_weight,
         top_bias.reshape(1, hidden_size),
-        out_weight.reshape(1, hidden_size),
+        out_weight,
     )
-    return logits.reshape(micro, local), grad_top, grad_bias.reshape(hidden_size)
+    return logits, grad_top, grad_bias.reshape(hidden_size)
 
 
 def solution(mesh):

time: 111 us -> 103 us (0.928)
  Pallas kernels: 106 us -> 97.4 us
    pallas_call x2 -> x1, Pallas kernels: 106 us -> 97.4 us  [per_device(): pl.pallas_call(functools.partial(step_kernel, samples_all), out_shape=(ja...]
    unnamed x12 -> x3, local copies, waits for them, and re-layouts: 2.41 us -> 4.81 us
    reshape x3 -> x0, local copies, waits for them, and re-layouts: 1.53 us -> none  [the longest x1 0.75 us: per_device(): out_weight.reshape(1, hidden_size)]
where the time goes in v1:
time: 103 us
  Pallas kernels  97.4 us (95%)
  local copies, waits for them, and re-layouts  4.81 us (5%)
    pallas_call x1, Pallas kernels, per_device(): pl.pallas_call(functools.partial(step_kernel, samples_all), out_shape=(ja...  97.4 us
    unnamed x3, local copies, waits for them, and re-layouts  4.81 us

profile of v1, /device:TPU:1, one launch (start us, length us, event | category | flops | bytes accessed | tf_op | source)
XLA Modules:
  0.0 102.9 jit_solution(10916644140303115942)
XLA Ops:
  0.6 97.4 %step.1 = (f32[4,32]{1,0:T(4,128)}, f32[256,1024]{1,0:T(8,128)}, f32[1,1024]{1,0:T(1,128)}) custom-call(s32[256]{0:T(256)} %slots_ref.1, s32[1,256]{1,0:T(1,128)} %bitcast.10, s32[128,2048]{1,0:T(8,128)} %bitcast.6, bf16[128,2048]{1,0:T(8,128)(2,1)} %bitcast.7, bf16[128,128]{1,0:T(8,128)(2,1)} %bitcast.8, bf16[8,1536,128]{2,1,0:T(8,128)(2,1)} %tables_hbm.1, ...), custom_call_target="tpu_custom_call" | custom-call | tf_op jit(solution)/shard_map/step/pallas_call | solution.py:483
  98.1 1.2 %copy.15 = f32[4,32]{1,0:T(4,128)} copy(f32[4,32]{1,0:T(4,128)} %get-tuple-element.12) | data formatting | bytes 1024
  99.3 2.3 %copy.16 = f32[256,1024]{1,0:T(8,128)} copy(f32[256,1024]{1,0:T(8,128)} %get-tuple-element.13) | data formatting | bytes 2097152
  101.6 1.3 %copy.17 = f32[1024]{0:T(1024)} copy(f32[1024]{0:T(1024)} %bitcast.11) | data formatting | bytes 8192

commit v2 on v1

--- a/solution.py
+++ b/solution.py
@@ -16,6 +16,10 @@
 Z_BIT = 4
 PLANE = 16
 ROWS = 128
+FIRST_NEAR = 8
+FIRST_FAR = 4
+FAR_RATE = 1
+PASS_AT = 4
 
 
 def place():
@@ -25,10 +29,6 @@
 
 def mirrored(grp):
     return (3 - grp // 2) * 2 + grp % 2
-
-
-def order(step):
-    return (step // 8) * 8 + (step % 2) * Z_BIT + (step // 2) % 4
 
 
 def plane(at):
@@ -135,7 +135,12 @@
             rows = slice(lines + pair * 2 * HOTS, lines + (pair + 1) * 2 * HOTS)
             target[offset, rows, :] = jnp.concatenate([weights_t[one], weights_t[two]], axis=0).astype(jnp.bfloat16)
 
+    def pack_all(offset, _):
+        packed(offset, send)
+        return 0
+
     packed(0, recv)
+    lax.fori_loop(1, peers, pack_all, 0)
     pl.semaphore_wait(barrier, peers - 1 + 7 + 1)
 
     def feature_copy(source, offset):
@@ -168,23 +173,56 @@
 
     feature_copy(features_ref, Z_BIT).start()
 
-    def send_features(m, _):
-        feature_copy(features_ref, order(2 * m)).start()
-        return 0
-
-    lax.fori_loop(1, PLANE, send_features, 0)
-
-
-    def send_payload(step, _):
-        offset = order(step)
-        packed(offset, send)
+    def send_near(at):
+        offset = plane(at)
+        feature_copy(features_ref, offset).start()
         payload_copy(offset).start()
-        return 0
-
-    lax.fori_loop(1, peers, send_payload, 0)
-    def pass_features(m, _):
-        passed_on(order(2 * m)).start()
-        return 0
+
+    def send_far(at):
+        offset = plane(at) + Z_BIT
+        payload_copy(offset).start()
+
+    def pass_features(at):
+        passed_on(plane(at)).start()
+
+    def first_sends(at, _):
+        @pl.when(at < FIRST_NEAR)
+        def _():
+            send_near(at)
+
+        @pl.when(at - 1 < FIRST_FAR)
+        def _():
+            send_far(at - 1)
+
+        return 0
+
+    lax.fori_loop(1, max(FIRST_NEAR, FIRST_FAR + 1), first_sends, 0)
+
+    def later_sends(m):
+        for side in range(2):
+            near = FIRST_NEAR + 2 * m + side
+
+            @pl.when(near < PLANE)
+            def _():
+                send_near(near)
+
+        for side in range(FAR_RATE):
+            far = FIRST_FAR + FAR_RATE * m + side
+
+            @pl.when(far < PLANE)
+            def _():
+                send_far(far)
+
+        @pl.when(m == PASS_AT)
+        def _():
+            feature_copy(features_ref, Z_BIT).wait_recv()
+
+        for side in range(2):
+            place_to = 1 + 2 * (m - PASS_AT) + side
+
+            @pl.when((m >= PASS_AT) & (place_to < PLANE))
+            def _():
+                pass_features(place_to)
 
     scale = 1.0 / math.sqrt(width)
     tile = 128
@@ -204,6 +242,7 @@
 
         payload_copy(both[1]).wait_recv()
         feature_copy(features_ref, both[1]).wait_recv()
+        later_sends(m)
         vectors = jnp.concatenate([feats[both[0]], feats[both[1]]], axis=0)
 
         for slot in range(own_slots):
@@ -244,11 +283,6 @@
             score_copy(both[0]).start()
 
         score_copy(both[1]).start()
-
-        @pl.when(m == 0)
-        def _():
-            feature_copy(features_ref, Z_BIT).wait_recv()
-            lax.fori_loop(1, PLANE, pass_features, 0)
 
         return 0
 
@@ -458,8 +492,8 @@
     feature_copy(features_ref, Z_BIT).wait_send()
 
     def finish_features(m, _):
-        feature_copy(features_ref, order(2 * m)).wait_send()
-        passed_on(order(2 * m)).wait_send()
+        feature_copy(features_ref, plane(m)).wait_send()
+        passed_on(plane(m)).wait_send()
         return 0
 
     lax.fori_loop(1, PLANE, finish_features, 0)

time: 103 us -> 98 us (0.951)
  Pallas kernels: 97.4 us -> 92.4 us
    pallas_call x1, Pallas kernels: 97.4 us -> 92.4 us  [per_device(): pl.pallas_call(functools.partial(step_kernel, samples_all), out_shape=(ja...]
where the time goes in v2:
time: 98 us; the launch traced here: 97.8 us
  Pallas kernels  92.4 us (94%)
  local copies, waits for them, and re-layouts  4.81 us (5%)
    pallas_call x1, Pallas kernels, per_device(): pl.pallas_call(functools.partial(step_kernel, samples_all), out_shape=(ja...  92.4 us
    unnamed x3, local copies, waits for them, and re-layouts  4.81 us

profile of v2, /device:TPU:1, one launch (start us, length us, event | category | flops | bytes accessed | tf_op | source)
XLA Modules:
  0.0 97.8 jit_solution(7286128282458945024)
XLA Ops:
  0.6 92.4 %step.1 = (f32[4,32]{1,0:T(4,128)}, f32[256,1024]{1,0:T(8,128)}, f32[1,1024]{1,0:T(1,128)}) custom-call(s32[256]{0:T(256)} %slots_ref.1, s32[1,256]{1,0:T(1,128)} %bitcast.10, s32[128,2048]{1,0:T(8,128)} %bitcast.6, bf16[128,2048]{1,0:T(8,128)(2,1)} %bitcast.7, bf16[128,128]{1,0:T(8,128)(2,1)} %bitcast.8, bf16[8,1536,128]{2,1,0:T(8,128)(2,1)} %tables_hbm.1, ...), custom_call_target="tpu_custom_call" | custom-call | tf_op jit(solution)/shard_map/step/pallas_call | solution.py:517
  93.0 1.2 %copy.15 = f32[4,32]{1,0:T(4,128)} copy(f32[4,32]{1,0:T(4,128)} %get-tuple-element.12) | data formatting | bytes 1024
  94.2 2.3 %copy.16 = f32[256,1024]{1,0:T(8,128)} copy(f32[256,1024]{1,0:T(8,128)} %get-tuple-element.13) | data formatting | bytes 2097152
  96.5 1.3 %copy.17 = f32[1024]{0:T(1024)} copy(f32[1024]{0:T(1024)} %bitcast.11) | data formatting | bytes 8192

commit v3 on v2

--- a/solution.py
+++ b/solution.py
@@ -16,7 +16,7 @@
 Z_BIT = 4
 PLANE = 16
 ROWS = 128
-FIRST_NEAR = 8
+FIRST_NEAR = 10
 FIRST_FAR = 4
 FAR_RATE = 1
 PASS_AT = 4
@@ -171,8 +171,6 @@
             device_id=peer_of(grp, tab, offset), device_id_type=MESH,
         )
 
-    feature_copy(features_ref, Z_BIT).start()
-
     def send_near(at):
         offset = plane(at)
         feature_copy(features_ref, offset).start()
@@ -185,18 +183,17 @@
     def pass_features(at):
         passed_on(plane(at)).start()
 
-    def first_sends(at, _):
-        @pl.when(at < FIRST_NEAR)
-        def _():
-            send_near(at)
-
-        @pl.when(at - 1 < FIRST_FAR)
-        def _():
-            send_far(at - 1)
-
-        return 0
-
-    lax.fori_loop(1, max(FIRST_NEAR, FIRST_FAR + 1), first_sends, 0)
+    def first_near(at, _):
+        send_near(at)
+        return 0
+
+    def first_far(at, _):
+        send_far(at)
+        return 0
+
+    lax.fori_loop(1, FIRST_NEAR, first_near, 0)
+    feature_copy(features_ref, Z_BIT).start()
+    lax.fori_loop(0, FIRST_FAR, first_far, 0)
 
     def later_sends(m):
         for side in range(2):

time: 98 us -> 98.8 us (level)
  no operation moved by 1% of the time
where the time goes in v3:
time: 98.8 us; the launch traced here: 98.6 us
  Pallas kernels  93.2 us (94%)
  local copies, waits for them, and re-layouts  4.81 us (5%)
    pallas_call x1, Pallas kernels, per_device(): pl.pallas_call(functools.partial(step_kernel, samples_all), out_shape=(ja...  93.2 us
    unnamed x3, local copies, waits for them, and re-layouts  4.81 us

profile of v3, /device:TPU:1, one launch (start us, length us, event | category | flops | bytes accessed | tf_op | source)
XLA Modules:
  0.0 98.6 jit_solution(1289071961162712260)
XLA Ops:
  0.6 93.2 %step.1 = (f32[4,32]{1,0:T(4,128)}, f32[256,1024]{1,0:T(8,128)}, f32[1,1024]{1,0:T(1,128)}) custom-call(s32[256]{0:T(256)} %slots_ref.1, s32[1,256]{1,0:T(1,128)} %bitcast.10, s32[128,2048]{1,0:T(8,128)} %bitcast.6, bf16[128,2048]{1,0:T(8,128)(2,1)} %bitcast.7, bf16[128,128]{1,0:T(8,128)(2,1)} %bitcast.8, bf16[8,1536,128]{2,1,0:T(8,128)(2,1)} %tables_hbm.1, ...), custom_call_target="tpu_custom_call" | custom-call | tf_op jit(solution)/shard_map/step/pallas_call | solution.py:514
  93.8 1.2 %copy.15 = f32[4,32]{1,0:T(4,128)} copy(f32[4,32]{1,0:T(4,128)} %get-tuple-element.12) | data formatting | bytes 1024
  95.0 2.3 %copy.16 = f32[256,1024]{1,0:T(8,128)} copy(f32[256,1024]{1,0:T(8,128)} %get-tuple-element.13) | data formatting | bytes 2097152
  97.3 1.3 %copy.17 = f32[1024]{0:T(1024)} copy(f32[1024]{0:T(1024)} %bitcast.11) | data formatting | bytes 8192

commit v4 on v2

--- a/solution.py
+++ b/solution.py
@@ -292,25 +292,6 @@
     for load in loads[4:]:
         load.wait()
 
-    def take_scores(offset, _):
-        score_copy(offset).wait_recv()
-        return 0
-
-    lax.fori_loop(1, peers, take_scores, 0)
-
-    core = grp % 2
-    xy = (tab // 8) * 4 + tab % 4
-    z = ((tab // Z_BIT) % 2) * 4 + grp // 2
-    tables, hidden_size = top_ref.shape
-    at_table = (lax.broadcasted_iota(jnp.int32, (tables, tables), 0) == slot_row[...]).astype(jnp.bfloat16)
-    scores_wide = jnp.dot(at_table, scores_ref[...].reshape(tables, LANES), preferred_element_type=jnp.float32)
-    scores_t = scores_wide.astype(jnp.bfloat16)
-    scores = scores_wide.T.astype(jnp.bfloat16)
-    pre = jnp.dot(scores, top_ref[...], preferred_element_type=jnp.float32) + bias_ref[...]
-    gate = jax.nn.sigmoid(pre)
-    hidden = (pre * gate).astype(jnp.bfloat16)
-    out_wide = out_ref[...].astype(jnp.float32).reshape(1, hidden_size)
-    logit_column = jnp.sum(hidden.astype(jnp.float32) * out_wide, axis=1, keepdims=True)
     micro, local = labels_ref.shape
     sample = lax.broadcasted_iota(jnp.int32, (LANES, local), 0)
     within = sample % local == lax.broadcasted_iota(jnp.int32, (LANES, local), 1)
@@ -321,33 +302,58 @@
     )
     own_batch = batch_of == lax.broadcasted_iota(jnp.int32, (LANES, micro), 1)
     labels = jnp.sum(jnp.where(own_batch, spread, 0.0), axis=1, keepdims=True)
+
+    def take_scores(offset, _):
+        score_copy(offset).wait_recv()
+        return 0
+
+    lax.fori_loop(1, peers, take_scores, 0)
+
+    core = grp % 2
+    xy = (tab // 8) * 4 + tab % 4
+    z = ((tab // Z_BIT) % 2) * 4 + grp // 2
+    tables, hidden_size = top_ref.shape
+    at_table = (lax.broadcasted_iota(jnp.int32, (tables, tables), 0) == slot_row[...]).astype(jnp.bfloat16)
+    scores_wide = jnp.dot(at_table, scores_ref[...].reshape(tables, LANES), preferred_element_type=jnp.float32)
+    scores = scores_wide.T.astype(jnp.bfloat16)
+    pre = jnp.dot(scores, top_ref[...], preferred_element_type=jnp.float32) + bias_ref[...]
+    gate = jax.nn.sigmoid(pre)
+    hidden = (pre * gate).astype(jnp.bfloat16)
+    out_wide = out_ref[...].astype(jnp.float32).reshape(1, hidden_size)
+    logit_column = jnp.sum(hidden.astype(jnp.float32) * out_wide, axis=1, keepdims=True)
+    delta = (jax.nn.sigmoid(logit_column) - labels) * (loss_scale / samples_all)
+    slope = gate * (1.0 + pre * (1.0 - gate))
+    hidden_grad_wide = delta * out_wide * slope
+    hidden_grad = hidden_grad_wide.astype(jnp.bfloat16)
+    other = pl.multiple_of((1 - core) * ROWS, ROWS)
+    mine = pl.multiple_of(core * ROWS, ROWS)
+
+    def to_partner(source, target, sems):
+        return pltpu.make_async_remote_copy(
+            src_ref=source, dst_ref=target, send_sem=sems.at[0], recv_sem=sems.at[1],
+            device_id=partner, device_id_type=MESH,
+        )
+
+    def half_grad(start):
+        at = lax.broadcasted_iota(jnp.int32, (ROWS, tables), 0) + start == slot_row[...]
+        rows = jnp.dot(
+            at.astype(jnp.bfloat16), scores_ref[...].reshape(tables, LANES), preferred_element_type=jnp.float32
+        ).astype(jnp.bfloat16)
+        return jnp.dot(rows, hidden_grad, preferred_element_type=jnp.float32)
+
+    bias_swap = to_partner(bias_part, bias_half, bhalf_sem)
+    half_swap = to_partner(half_send, half_recv, half_sem)
+    bias_part[...] = jnp.sum(hidden_grad.astype(jnp.float32), axis=0, keepdims=True)
+    bias_swap.start()
+    half_send[...] = half_grad(other).reshape(16, 8, hidden_size).astype(jnp.bfloat16)
+    half_swap.start()
+    grad[...] = half_grad(mine)
     rows_of = lax.broadcasted_iota(jnp.int32, (micro, LANES), 1) // local
     picks = (rows_of == lax.broadcasted_iota(jnp.int32, (micro, LANES), 0)).astype(jnp.float32)
     logits_ref[...] = jnp.dot(
         picks, jnp.where(within, logit_column, 0.0),
         precision=lax.Precision.HIGHEST, preferred_element_type=jnp.float32,
     )
-    delta = (jax.nn.sigmoid(logit_column) - labels) * (loss_scale / samples_all)
-    slope = gate * (1.0 + pre * (1.0 - gate))
-    hidden_grad_wide = delta * out_wide * slope
-    hidden_grad = hidden_grad_wide.astype(jnp.bfloat16)
-    grad[...] = jnp.dot(scores_t, hidden_grad, preferred_element_type=jnp.float32)
-    bias_part[...] = jnp.sum(hidden_grad.astype(jnp.float32), axis=0, keepdims=True)
-
-    other = pl.multiple_of((1 - core) * ROWS, ROWS)
-    mine = pl.multiple_of(core * ROWS, ROWS)
-    half_send[...] = grad[pl.ds(other, ROWS), :].reshape(16, 8, hidden_size).astype(jnp.bfloat16)
-
-    def to_partner(source, target, sems):
-        return pltpu.make_async_remote_copy(
-            src_ref=source, dst_ref=target, send_sem=sems.at[0], recv_sem=sems.at[1],
-            device_id=partner, device_id_type=MESH,
-        )
-
-    bias_swap = to_partner(bias_part, bias_half, bhalf_sem)
-    half_swap = to_partner(half_send, half_recv, half_sem)
-    bias_swap.start()
-    half_swap.start()
     bias_swap.wait()
     bias_sum[...] = bias_part[...] + bias_half[...]
     bias_plane[pl.ds(xy, 1)] = bias_sum[...][None]
@@ -371,7 +377,7 @@
     def fold(k):
         row = pl.multiple_of(flip(xy, k, 4) * 8, 8)
         wide = half_recv[pl.ds(flip(xy, k, 4), 1)][0].astype(jnp.float32)
-        return grad[pl.ds(pl.multiple_of(mine + row, 8), 8), :] + wide
+        return grad[pl.ds(row, 8), :] + wide
 
     def send_plane(k, _):
         plane_send[k] = fold(k).astype(jnp.bfloat16)
@@ -541,7 +547,7 @@
             pltpu.VMEM((peers, own_slots, count), bf16),
             pltpu.VMEM((2, own_slots, count), f32),
             pltpu.VMEM((peers, own_slots, count), bf16),
-            pltpu.VMEM((tables, hidden_size), f32),
+            pltpu.VMEM((ROWS, hidden_size), f32),
             pltpu.VMEM((16, 8, hidden_size), bf16),
             pltpu.VMEM((16, 8, hidden_size), bf16),
             pltpu.VMEM((16, 8, hidden_size), bf16),

time: 98 us -> 97.9 us (level)
  no operation moved by 1% of the time
where the time goes in v4:
time: 97.9 us; the launch traced here: 97.7 us
  Pallas kernels  92.3 us (94%)
  local copies, waits for them, and re-layouts  4.81 us (5%)
    pallas_call x1, Pallas kernels, per_device(): pl.pallas_call(functools.partial(step_kernel, samples_all), out_shape=(ja...  92.3 us
    unnamed x3, local copies, waits for them, and re-layouts  4.81 us

profile of v4, /device:TPU:1, one launch (start us, length us, event | category | flops | bytes accessed | tf_op | source)
XLA Modules:
  0.0 97.7 jit_solution(13874649192314514572)
XLA Ops:
  0.6 92.3 %step.1 = (f32[4,32]{1,0:T(4,128)}, f32[256,1024]{1,0:T(8,128)}, f32[1,1024]{1,0:T(1,128)}) custom-call(s32[256]{0:T(256)} %slots_ref.1, s32[1,256]{1,0:T(1,128)} %bitcast.10, s32[128,2048]{1,0:T(8,128)} %bitcast.6, bf16[128,2048]{1,0:T(8,128)(2,1)} %bitcast.7, bf16[128,128]{1,0:T(8,128)(2,1)} %bitcast.8, bf16[8,1536,128]{2,1,0:T(8,128)(2,1)} %tables_hbm.1, ...), custom_call_target="tpu_custom_call" | custom-call | tf_op jit(solution)/shard_map/step/pallas_call | solution.py:523
  92.9 1.2 %copy.15 = f32[4,32]{1,0:T(4,128)} copy(f32[4,32]{1,0:T(4,128)} %get-tuple-element.12) | data formatting | bytes 1024
  94.2 2.3 %copy.16 = f32[256,1024]{1,0:T(8,128)} copy(f32[256,1024]{1,0:T(8,128)} %get-tuple-element.13) | data formatting | bytes 2097152
  96.5 1.3 %copy.17 = f32[1024]{0:T(1024)} copy(f32[1024]{0:T(1024)} %bitcast.11) | data formatting | bytes 8192
